TPU v7x, 256 devices: a whole 4x4x8 slice. The times are simulated.
256 devices in a mesh: row: 8 (over y, core), col: 32 (over x, z).
Axes of the slice: x: 4, y: 4, z: 8, core: 2. Of those that a mesh axis runs over, the one named last changes fastest.
Arguments:
- phases: int32 [8, 32, 8, 24, 576], P('row', 'col'), may hold values from 0 to 2
- grain: float32 [8, 32, 8, 24, 576], P('row', 'col'), may hold values from 0.5 to 2
- phase_cond: float32 [3], replicated, may hold values from 0.3 to 3
- micro_counts: int32 [8, 32, 8], P('row', 'col'), may hold values from 6 to 12, as said below
- current: float32 [8, 32, 8], P('row', 'col'), may hold values from -5 to 5
- load: float32 [8, 32, 8], P('row', 'col'), may hold values from -16 to 16
Outputs:
- states: float32 [8, 32, 8, 3, 24, 576], P('row', 'col')
- tangent: float32 [8, 32, 8, 3, 3], P('row', 'col')
- increment: float32 [8, 32, 8], P('row', 'col')
- residual: float32 [8, 32, 8], P('row', 'col')
Inputs may be any that keep to these rules, and one draw needn't show every extreme that they name: `micro_counts`: every draw has an element with 12 inner iterations and one with 6.
All inputs are finite; a program needn't handle non-finite values.
Results may differ from a plain program's by a relative error of at most 0.0003.
Values sent between devices are 32-bit elements; how exact they have to be, the bound alone decides.
A program may use at most 64 MiB of HBM per device.

v0:
```python
import jax
import jax.numpy as jnp
from jax import lax
from jax.sharding import Mesh
from jax.sharding import PartitionSpec as P

VOX = 24
YZ = 576
PHASES = 3
MACRO_ITERS = 8
ROW_COL = ("row_0", "row_1", "col_0", "col_1")
ROW = ("row_0", "row_1")
COL = ("col_0", "col_1")


def laid_out(pieces, dim):
    pieces = jnp.moveaxis(pieces, 0, dim)
    shape = pieces.shape
    return pieces.reshape(*shape[:dim], shape[dim] * shape[dim + 1], *shape[dim + 2 :])


def gather_in_order(shard, axes, turns):
    pieces = shard
    for k in turns:
        pieces = lax.all_gather(pieces, axes[k])
    done = turns[::-1]
    back = [done.index(k) for k in range(len(axes))]
    pieces = pieces.transpose(*back, *range(len(axes), pieces.ndim))
    return pieces.reshape(-1, *shard.shape)


def whole_of(shard, axes, turns, dim):
    return laid_out(gather_in_order(shard, axes, turns), dim)


def forward(field, axis_id):
    z_index = jnp.arange(YZ) % VOX
    if axis_id == 0:
        return jnp.roll(field, -1, axis=-2)
    if axis_id == 1:
        return jnp.roll(field, -VOX, axis=-1)
    return jnp.where(
        z_index == VOX - 1, jnp.roll(field, VOX - 1, axis=-1), jnp.roll(field, -1, axis=-1)
    )


def behind(field, axis_id):
    z_index = jnp.arange(YZ) % VOX
    if axis_id == 0:
        return jnp.roll(field, 1, axis=-2)
    if axis_id == 1:
        return jnp.roll(field, VOX, axis=-1)
    return jnp.where(z_index == 0, jnp.roll(field, 1 - VOX, axis=-1), jnp.roll(field, 1, axis=-1))


def solve_rve(conduct, count):
    faces = [(conduct + forward(conduct, axis_id)) * 0.5 for axis_id in range(3)]
    back_faces = [behind(faces[axis_id], axis_id) for axis_id in range(3)]
    rhs = jnp.stack([faces[axis_id] - back_faces[axis_id] for axis_id in range(3)])

    def operate(field):
        total = jnp.zeros_like(field)
        for axis_id in range(3):
            total = total + faces[axis_id] * (field - forward(field, axis_id))
            total = total + back_faces[axis_id] * (field - behind(field, axis_id))
        return total

    def sweep(index, carry):
        fluct, remain, direction, norm_now = carry
        image = operate(direction)
        step_size = norm_now / jnp.sum(direction * image, axis=(1, 2))
        fluct = fluct + step_size[:, None, None] * direction
        remain = remain - step_size[:, None, None] * image
        norm_next = jnp.sum(remain * remain, axis=(1, 2))
        direction = remain + (norm_next / norm_now)[:, None, None] * direction
        return (fluct, remain, direction, norm_next)

    start = (jnp.zeros_like(rhs), rhs, rhs, jnp.sum(rhs * rhs, axis=(1, 2)))
    fluct = lax.fori_loop(0, count, sweep, start)[0]
    identity = jnp.eye(3, dtype=conduct.dtype)
    rows_out = []
    for axis_id in range(3):
        flux = faces[axis_id][None] * (
            identity[axis_id][:, None, None] + forward(fluct, axis_id) - fluct
        )
        rows_out.append(jnp.mean(flux, axis=(1, 2)))
    return (fluct, jnp.stack(rows_out))


def solve_batch(conduct, counts):
    return lax.map(lambda pair: solve_rve(pair[0], pair[1]), (conduct, counts))


def neighbour(padded, axis_id, offset):
    lead = padded.ndim - 3
    index = [slice(None)] * lead + [slice(1, -1)] * 3
    length = padded.shape[lead + axis_id]
    index[lead + axis_id] = slice(1 + offset, length - 1 + offset)
    return padded[tuple(index)]


def coarse_apply(k_padded, v_padded):
    centre = neighbour(v_padded, 0, 0)
    total = jnp.zeros_like(centre)
    for axis_id in range(3):
        k_centre = neighbour(k_padded[axis_id], 0, 0)
        for offset in (1, -1):
            cond_face = 0.5 * (k_centre + neighbour(k_padded[axis_id], axis_id, offset))
            total = total + cond_face * (centre - neighbour(v_padded, axis_id, offset))
    return total


def coarse_cg(k_padded, residual, pad_field, norm_of, curv_of):
    increment = jnp.zeros_like(residual)
    direction = residual
    norm_now = norm_of(residual)
    for iteration in range(MACRO_ITERS):
        image = coarse_apply(k_padded, pad_field(direction))
        step_size = norm_now / curv_of(direction, image)
        increment = increment + step_size * direction
        residual = residual - step_size * image
        norm_next = norm_of(residual)
        direction = residual + norm_next / norm_now * direction
        norm_now = norm_next
    return (increment, residual)


def local_norm(field):
    return jnp.sum(field * field)


def local_curv(first, second):
    return jnp.sum(first * second)


def shards(phases, grain, phase_cond, micro_counts, current, load):
    depth = phases.shape[2]
    conduct = jnp.zeros(grain.shape, grain.dtype)
    for phase_id in range(PHASES):
        conduct = conduct + jnp.where(phases == phase_id, phase_cond[phase_id], 0.0)
    conduct = conduct * grain
    flat = conduct.reshape(depth, VOX, YZ)
    counts = micro_counts.reshape(depth)
    fluct, tangent = solve_batch(flat, counts)
    states = fluct.reshape(1, 1, depth, 3, VOX, YZ)
    tangent_out = tangent.reshape(1, 1, depth, 3, 3)
    diag = jnp.stack([tangent[:, axis_id, axis_id] for axis_id in range(3)]).reshape(3, 1, 1, depth)
    packed = jnp.concatenate(
        [diag, current.reshape(1, 1, 1, depth), load.reshape(1, 1, 1, depth)], axis=0
    ).reshape(5, 1, depth)
    whole = whole_of(packed, ROW_COL, (0, 2, 3, 1), 1)
    whole = whole.reshape(5, lax.axis_size(ROW), lax.axis_size(COL), depth)
    padded = jnp.pad(whole, ((0, 0), (1, 1), (1, 1), (1, 1)))
    residual = whole[4] - coarse_apply(padded[:3], padded[3])
    increment, residual = coarse_cg(
        padded[:3], residual, lambda field: jnp.pad(field, 1), local_norm, local_curv
    )
    row_at = lax.axis_index(ROW)
    col_at = lax.axis_index(COL)
    zero_at = jnp.zeros((), jnp.int32)
    increment = lax.dynamic_slice(increment, (row_at, col_at, zero_at), (1, 1, depth))
    residual = lax.dynamic_slice(residual, (row_at, col_at, zero_at), (1, 1, depth))
    return (states, tangent_out, increment, residual)


def solution(mesh):
    torus = Mesh(mesh.devices.reshape(4, 2, 4, 8), ("row_0", "row_1", "col_0", "col_1"))
    in_specs = (
        P(ROW, COL, None, None, None),
        P(ROW, COL, None, None, None),
        P(),
        P(ROW, COL, None),
        P(ROW, COL, None),
        P(ROW, COL, None),
    )
    out_specs = (
        P(ROW, COL, None, None, None, None),
        P(ROW, COL, None, None, None),
        P(ROW, COL, None),
        P(ROW, COL, None),
    )
    return jax.shard_map(
        shards, mesh=torus, in_specs=in_specs, out_specs=out_specs, check_vma=False
    )
```

profile of v0, /device:TPU:1, one launch (start us, length us, event | category | flops | bytes accessed | tf_op | source)
XLA Modules:
  0.0 326.8 jit_solution(15595284607173324453)
XLA Ops:
  0.6 1.4 fusion.241
  2.0 3.3 multiply_bitcast_fusion.3
  5.3 149.6 %while.43 = (s32[]{:T(128)}, f32[8,3,24,576]{3,2,1,0:T(8,128)S(1)}, f32[8,3,3]{2,1,0:T(4,128)S(1)}, f32[8,24,576]{2,1,0:T(8,128)S(1)}, s32[8]{0:T(128)S(1)}, /*i...) while((s32[]{:T(128)}, f32[8,3,24,576]{3,2,1,0:T(8,128)S(1)}, f32[8,3,3]{2,1,0:T(4,128)S(1)}, ...), condition=%wide.region_9.10_spmd, body=%wide.region_0.9_spmd.sunk | while | flops 2898470 | bytes 12391870 | solution.py:91
  7.3 17.8 %while.44 = (s32[]{:T(128)}, f32[3,24,576]{2,1,0:T(8,128)S(1)}, f32[3,24,576]{2,1,0:T(8,128)S(1)}, f32[3,24,576]{2,1,0:T(8,128)S(1)}, f32[3]{0:T(128)S(1)}, /*in...) while((s32[]{:T(128)}, f32[3,24,576]{2,1,0:T(8,128)S(1)}, ...), condition=%wide.region_5.5_spmd, body=%wide.region_2.4_spmd.sunk | while | flops 1539074 | bytes 5974553 | solution.py:79
  27.9 13.5 %while.44 = (s32[]{:T(128)}, f32[3,24,576]{2,1,0:T(8,128)S(1)}, f32[3,24,576]{2,1,0:T(8,128)S(1)}, f32[3,24,576]{2,1,0:T(8,128)S(1)}, f32[3]{0:T(128)S(1)}, /*in...) while((s32[]{:T(128)}, f32[3,24,576]{2,1,0:T(8,128)S(1)}, ...), condition=%wide.region_5.5_spmd, body=%wide.region_2.4_spmd.sunk | while | flops 1539074 | bytes 5974553 | solution.py:79
  44.2 17.8 %while.44 = (s32[]{:T(128)}, f32[3,24,576]{2,1,0:T(8,128)S(1)}, f32[3,24,576]{2,1,0:T(8,128)S(1)}, f32[3,24,576]{2,1,0:T(8,128)S(1)}, f32[3]{0:T(128)S(1)}, /*in...) while((s32[]{:T(128)}, f32[3,24,576]{2,1,0:T(8,128)S(1)}, ...), condition=%wide.region_5.5_spmd, body=%wide.region_2.4_spmd.sunk | while | flops 1539074 | bytes 5974553 | solution.py:79
  64.8 17.8 %while.44 = (s32[]{:T(128)}, f32[3,24,576]{2,1,0:T(8,128)S(1)}, f32[3,24,576]{2,1,0:T(8,128)S(1)}, f32[3,24,576]{2,1,0:T(8,128)S(1)}, f32[3]{0:T(128)S(1)}, /*in...) while((s32[]{:T(128)}, f32[3,24,576]{2,1,0:T(8,128)S(1)}, ...), condition=%wide.region_5.5_spmd, body=%wide.region_2.4_spmd.sunk | while | flops 1539074 | bytes 5974553 | solution.py:79
  85.4 17.8 %while.44 = (s32[]{:T(128)}, f32[3,24,576]{2,1,0:T(8,128)S(1)}, f32[3,24,576]{2,1,0:T(8,128)S(1)}, f32[3,24,576]{2,1,0:T(8,128)S(1)}, f32[3]{0:T(128)S(1)}, /*in...) while((s32[]{:T(128)}, f32[3,24,576]{2,1,0:T(8,128)S(1)}, ...), condition=%wide.region_5.5_spmd, body=%wide.region_2.4_spmd.sunk | while | flops 1539074 | bytes 5974553 | solution.py:79
  105.9 13.5 %while.44 = (s32[]{:T(128)}, f32[3,24,576]{2,1,0:T(8,128)S(1)}, f32[3,24,576]{2,1,0:T(8,128)S(1)}, f32[3,24,576]{2,1,0:T(8,128)S(1)}, f32[3]{0:T(128)S(1)}, /*in...) while((s32[]{:T(128)}, f32[3,24,576]{2,1,0:T(8,128)S(1)}, ...), condition=%wide.region_5.5_spmd, body=%wide.region_2.4_spmd.sunk | while | flops 1539074 | bytes 5974553 | solution.py:79
  122.2 15.7 %while.44 = (s32[]{:T(128)}, f32[3,24,576]{2,1,0:T(8,128)S(1)}, f32[3,24,576]{2,1,0:T(8,128)S(1)}, f32[3,24,576]{2,1,0:T(8,128)S(1)}, f32[3]{0:T(128)S(1)}, /*in...) while((s32[]{:T(128)}, f32[3,24,576]{2,1,0:T(8,128)S(1)}, ...), condition=%wide.region_5.5_spmd, body=%wide.region_2.4_spmd.sunk | while | flops 1539074 | bytes 5974553 | solution.py:79
  140.7 13.5 %while.44 = (s32[]{:T(128)}, f32[3,24,576]{2,1,0:T(8,128)S(1)}, f32[3,24,576]{2,1,0:T(8,128)S(1)}, f32[3,24,576]{2,1,0:T(8,128)S(1)}, f32[3]{0:T(128)S(1)}, /*in...) while((s32[]{:T(128)}, f32[3,24,576]{2,1,0:T(8,128)S(1)}, ...), condition=%wide.region_5.5_spmd, body=%wide.region_2.4_spmd.sunk | while | flops 1539074 | bytes 5974553 | solution.py:79
  155.2 9.8 %all-gather = f32[20,1,1,8]{3,2,1,0:T(1,128)S(1)} all-gather(f32[5,1,1,8]{3,2,1,0:T(1,128)S(1)} %copy.64), channel_id=2, replica_groups=mesh['row_0'=4,'row_1'=2,'col_0'=4,'col_1'=8] {'row_0'}, dimensions={0}, use_global_device_ids=true | all-gather | bytes 800 | tf_op jit(solution)/shard_map/all_gather | solution.py:25
  165.1 89.6 %all-gather.1 = f32[16,5,1,8]{3,2,1,0:T(1,128)S(1)} all-gather(f32[4,5,1,8]{3,2,1,0:T(1,128)S(1)} %bitcast.148), channel_id=3, replica_groups=mesh['row_0'=4,'row_1'=2,'col_0'=4,'col_1'=8] {'col_0'}, dimensions={0}, use_global_device_ids=true | all-gather | bytes 3200 | tf_op jit(solution)/shard_map/all_gather | solution.py:25
  254.7 22.8 %all-gather.2 = f32[32,4,5,1,8]{4,1,3,2,0:T(4,128)S(1)} all-gather(f32[4,4,5,1,8]{4,1,3,2,0:T(4,128)S(1)} %copy.65), channel_id=4, replica_groups=mesh['row_0'=4,'row_1'=2,'col_0'=4,'col_1'=8] {'col_1'}, dimensions={0}, use_global_device_ids=true | all-gather | bytes 23040 | tf_op jit(solution)/shard_map/all_gather | solution.py:25
  277.5 15.1 %all-gather.3 = f32[16,4,4,5,1,8]{5,1,0,3,2,4:T(4,128)S(1)} all-gather(f32[8,4,4,5,1,8]{5,1,0,3,2,4:T(4,128)S(1)} %bitcast.143), channel_id=5, replica_groups=mesh['row_0'=4,'row_1'=2,'col_0'=4,'col_1'=8] {'row_1'}, dimensions={0}, use_global_device_ids=true | all-gather | bytes 61440 | tf_op jit(solution)/shard_map/all_gather | solution.py:25
  294.8 0.7 multiply_reduce_fusion.17
  298.8 0.7 multiply_reduce_fusion.15
  302.8 0.7 multiply_reduce_fusion.13
  306.8 0.7 multiply_reduce_fusion.11
  310.8 0.7 multiply_reduce_fusion.9
  314.8 0.7 multiply_reduce_fusion.7
  318.8 0.7 multiply_reduce_fusion.5
  322.8 0.7 multiply_reduce_fusion.3
  326.1 0.7 copy.71
  (1257 shorter events, 109.0 us)
Async XLA Ops:
  0.6 4.7 %copy-start.3 = (s32[1,1,8]{2,1,0:T(1,128)S(1)}, s32[1,1,8]{2,1,0:T(1,128)}, u32[]{:S(2)}) copy-start(s32[1,1,8]{2,1,0:T(1,128)} %param.13) | copy-start | bytes 100
  5.3 149.9 %copy-start = (f32[1,1,8]{2,1,0:T(1,128)S(1)}, f32[1,1,8]{2,1,0:T(1,128)}, u32[]{:S(2)}) copy-start(f32[1,1,8]{2,1,0:T(1,128)} %param.15) | copy-start | bytes 100
  5.3 149.9 %copy-start.1 = (f32[1,1,8]{2,1,0:T(1,128)S(1)}, f32[1,1,8]{2,1,0:T(1,128)}, u32[]{:S(2)}) copy-start(f32[1,1,8]{2,1,0:T(1,128)} %param.14) | copy-start | bytes 100
  155.0 138.1 %copy-start.2 = (f32[8,3,24,576]{3,2,1,0:T(8,128)}, f32[8,3,24,576]{3,2,1,0:T(8,128)S(1)}, u32[]{:S(2)}) copy-start(f32[8,3,24,576]{3,2,1,0:T(8,128)S(1)} %get-tuple-element.269) | copy-start | bytes 3981316
where the time goes:
time: 328 us; the launch traced here: 327 us
  blocking collectives  137 us (42%)
  other arithmetic  67.7 us (21%)
  local copies, waits for them, and re-layouts  52.2 us (16%)
  loops' own time  48.6 us (15%)
  between operations  21 us (6%)
    all_gather x4, blocking collectives, gather_in_order(): pieces = lax.all_gather(pieces, axes[k])  137 us
    another operation x8, loops' own time, solve_rve(): fluct = lax.fori_loop(0, count, sweep, start)[0]  46.5 us
    reduce_sum x57, other arithmetic, sweep(): step_size = norm_now / jnp.sum(direction * image, axis=(1, 2))  24.1 us
    reduce_sum x57, other arithmetic, sweep(): norm_next = jnp.sum(remain * remain, axis=(1, 2))  13.5 us
    slice x130, local copies, waits for them, and re-layouts, forward(): return jnp.roll(field, -VOX, axis=-1)  11.7 us
    slice x130, local copies, waits for them, and re-layouts, forward(): jnp.roll(field, -1, axis=-1)  11.2 us
    slice x122, local copies, waits for them, and re-layouts, forward(): jnp.roll(field, VOX - 1, axis=-1)  11.2 us
    add x57, other arithmetic, sweep(): direction = remain + (norm_next / norm_now)[:, None, None] * direction  7.41 us

commit v1 on v0

v1 whole, which is shorter than its diff:
```python
import functools

import jax
import jax.numpy as jnp
from jax import lax
from jax.experimental import pallas as pl
from jax.experimental.pallas import tpu as pltpu
from jax.sharding import PartitionSpec as P

VOX = 24
YZ = 576
PHASES = 3
EZ = 8
MICRO_MAX = 12
MACRO_ITERS = 8
NX = 12
PLANE = 9
CELLS = NX * PLANE
ROWS = EZ * VOX
F32 = jnp.float32
BF16 = jnp.bfloat16
MESH = pl.DeviceIdType.MESH


def lane_iota():
    return lax.broadcasted_iota(jnp.int32, (8, 128), 1)


def roll(v, shift):
    return pltpu.roll(v, shift % 128, 1)


class Shifts:
    def __init__(self):
        lane = lane_iota()
        ys = (lane >> 3) & 7
        zs = lane & 7
        self.y_last, self.y_first = ys == 7, ys == 0
        self.z_last, self.z_first = zs == 7, zs == 0
        self.low = lane < 64

    def x_swap(self, v):
        return roll(v, 64)

    def y_up(self, v):
        return jnp.where(self.y_last, roll(v, 56), roll(v, -8))

    def y_down(self, v):
        return jnp.where(self.y_first, roll(v, -56), roll(v, 8))

    def z_up(self, v):
        return jnp.where(self.z_last, roll(v, 7), roll(v, -1))

    def z_down(self, v):
        return jnp.where(self.z_first, roll(v, -7), roll(v, 1))


def pieces(v, count):
    out = []
    for _ in range(count - 1):
        part = v.astype(BF16)
        out.append(part)
        v = v - part.astype(F32)
    out.append(v.astype(BF16))
    return out


def permutation():
    col = lax.broadcasted_iota(jnp.int32, (YZ, YZ), 1)
    row = lax.broadcasted_iota(jnp.int32, (YZ, YZ), 0)
    group = col >> 6
    y_in = (group * 11) >> 5
    z_in = group - 3 * y_in
    source = (((col >> 3) & 7) * 3 + y_in) * VOX + (col & 7) * 3 + z_in
    return jnp.where(row == source, 1.0, 0.0).astype(BF16)


def total(v):
    return jnp.broadcast_to(jnp.sum(v, axis=1, keepdims=True), (8, 128))


def micro_kernel(
    cond_ref, counts_ref, current_ref, load_ref, phases_ref, grain_ref,
    states_ref, tangent_ref, packed_ref,
    perm, stage, face, rhs, fluct, remain, direct, image, edge,
):
    sh = Shifts()
    cells = [(x, y, z) for x in range(NX) for y in range(3) for z in range(3)]

    def at(x, y, z):
        return x * PLANE + y * 3 + z

    perm[...] = permutation()
    phases = phases_ref[...].reshape(ROWS, YZ)
    conduct = jnp.zeros((ROWS, YZ), F32)
    for phase_id in range(PHASES):
        conduct = jnp.where(phases == phase_id, cond_ref[phase_id], conduct)
    conduct = conduct * grain_ref[...].reshape(ROWS, YZ)
    parts = jnp.concatenate(pieces(conduct, 3), axis=0)
    moved = jnp.dot(parts, perm[...], preferred_element_type=F32)
    moved = (moved[2 * ROWS :] + moved[ROWS : 2 * ROWS]) + moved[:ROWS]
    for j in range(4):
        stage[j, 0:ROWS, :] = moved[:, 128 * j : 128 * j + 128]
    stage[4, 0:ROWS, 0:64] = moved[:, 512:576]

    for x in range(NX):
        for j in range(5):
            low = stage[j, pl.ds(x, 8, stride=VOX), :]
            high = stage[j, pl.ds(x + NX, 8, stride=VOX), :]
            image[x * PLANE + 2 * j] = jnp.where(sh.low, low, roll(high, 64))
            if j < 4:
                image[x * PLANE + 2 * j + 1] = jnp.where(sh.low, roll(low, 64), high)

    for x, y, z in cells:
        t = at(x, y, z)
        here = image[t]
        ahead = image[t + PLANE] if x < NX - 1 else sh.x_swap(image[at(0, y, z)])
        face[t] = (here + ahead) * 0.5
        ahead = image[t + 3] if y < 2 else sh.y_up(image[at(x, 0, z)])
        face[CELLS + t] = (here + ahead) * 0.5
        ahead = image[t + 1] if z < 2 else sh.z_up(image[at(x, y, 0)])
        face[2 * CELLS + t] = (here + ahead) * 0.5

    zero = jnp.zeros((8, 128), F32)
    norms = [zero] * 3
    means = [zero] * 3
    for x, y, z in cells:
        t = at(x, y, z)
        back = [
            face[t - PLANE] if x > 0 else sh.x_swap(face[at(NX - 1, y, z)]),
            face[CELLS + t - 3] if y > 0 else sh.y_down(face[CELLS + at(x, 2, z)]),
            face[2 * CELLS + t - 1] if z > 0 else sh.z_down(face[2 * CELLS + at(x, y, 2)]),
        ]
        for c in range(3):
            here = face[c * CELLS + t]
            value = here - back[c]
            rhs[c * CELLS + t] = value
            remain[c * CELLS + t] = value
            direct[c * CELLS + t] = zero
            fluct[c * CELLS + t] = zero
            norms[c] = norms[c] + value * value
            means[c] = means[c] + here

    sub = lax.broadcasted_iota(jnp.int32, (8, 128), 0)
    counts = jnp.zeros((8, 128), jnp.int32)
    for k in range(EZ):
        counts = jnp.where(sub == k, counts_ref[k], counts)

    def sweep(index, carry):
        norm, alpha, beta = carry
        new_alpha, new_norm, new_beta = [], [], []
        for c in range(3):
            base = c * CELLS

            def renew(x):
                plane = {}
                for y in range(3):
                    for z in range(3):
                        t = base + at(x, y, z)
                        old = direct[t]
                        fluct[t] = fluct[t] + alpha[c] * old
                        plane[y, z] = remain[t] + beta[c] * old
                        direct[t] = plane[y, z]
                return plane

            last = renew(NX - 1)
            here = renew(0)
            before = {}
            for y in range(3):
                for z in range(3):
                    flux = face[at(NX - 1, y, z)] * (last[y, z] - sh.x_swap(here[y, z]))
                    edge[c * PLANE + y * 3 + z] = flux
                    before[y, z] = sh.x_swap(flux)
            acc = zero
            for x in range(NX):
                if x < NX - 2:
                    ahead = renew(x + 1)
                elif x == NX - 2:
                    ahead = {(y, z): direct[base + at(x + 1, y, z)] for y in range(3) for z in range(3)}
                flux_x, flux_y, flux_z = {}, {}, {}
                for y in range(3):
                    for z in range(3):
                        t = at(x, y, z)
                        v = here[y, z]
                        if x < NX - 1:
                            flux_x[y, z] = face[t] * (v - ahead[y, z])
                        else:
                            flux_x[y, z] = edge[c * PLANE + y * 3 + z]
                        up = here[y + 1, z] if y < 2 else sh.y_up(here[0, z])
                        flux_y[y, z] = face[CELLS + t] * (v - up)
                        up = here[y, z + 1] if z < 2 else sh.z_up(here[y, 0])
                        flux_z[y, z] = face[2 * CELLS + t] * (v - up)
                for y in range(3):
                    for z in range(3):
                        t = base + at(x, y, z)
                        down_y = flux_y[y - 1, z] if y > 0 else sh.y_down(flux_y[2, z])
                        down_z = flux_z[y, z - 1] if z > 0 else sh.z_down(flux_z[y, 2])
                        out = (flux_x[y, z] - before[y, z]) + ((flux_y[y, z] - down_y) + (flux_z[y, z] - down_z))
                        image[t] = out
                        acc = acc + here[y, z] * out
                before, here = flux_x, ahead
            step = norm[c] / total(acc)
            new_alpha.append(jnp.where(index < counts, step, 0.0))
        for c in range(3):
            base = c * CELLS
            acc = zero
            for t in range(base, base + CELLS):
                value = remain[t] - new_alpha[c] * image[t]
                remain[t] = value
                acc = acc + value * value
            fresh = total(acc)
            new_norm.append(fresh)
            new_beta.append(fresh / norm[c])
        return tuple(new_norm), tuple(new_alpha), tuple(new_beta)

    norm = tuple(total(v) for v in norms)
    norm, alpha, beta = lax.fori_loop(0, MICRO_MAX, sweep, (norm, (zero,) * 3, (zero,) * 3))

    inner = [[zero] * 3 for _ in range(3)]
    for t in range(CELLS):
        for c in range(3):
            value = fluct[c * CELLS + t] + alpha[c] * direct[c * CELLS + t]
            fluct[c * CELLS + t] = value
            for d in range(3):
                inner[d][c] = inner[d][c] + value * rhs[d * CELLS + t]
    scale = 1.0 / (VOX * YZ)
    tangent = [
        [(total(means[d] - inner[d][c]) if d == c else -total(inner[d][c])) * scale for c in range(3)]
        for d in range(3)
    ]
    lane = lane_iota()
    for d in range(3):
        rows = jnp.where(lane == 0, tangent[d][0], jnp.where(lane == 1, tangent[d][1], tangent[d][2]))
        tangent_ref[:, d, :] = rows[:, 0:3]

    slot = lane >> 3
    message = jnp.where(slot == 0, tangent[0][0], jnp.where(slot == 1, tangent[1][1], tangent[2][2]))
    message = jnp.where((sub == (lane & 7)) & (slot < 3), message, 0.0)
    message = jnp.sum(message, axis=0, keepdims=True)
    low = lax.broadcasted_iota(jnp.int32, (1, 128), 1)
    for k in range(EZ):
        message = jnp.where(low == 24 + k, current_ref[k], message)
        message = jnp.where(low == 32 + k, load_ref[k], message)
    packed_ref[...] = message

    for c in range(3):
        for x in range(NX):
            for j in range(5):
                first = fluct[c * CELLS + x * PLANE + 2 * j]
                second = fluct[c * CELLS + x * PLANE + 2 * j + 1] if j < 4 else zero
                stage[j, pl.ds(c * ROWS + x, 8, stride=VOX), :] = jnp.where(sh.low, first, roll(second, 64))
                stage[j, pl.ds(c * ROWS + x + NX, 8, stride=VOX), :] = jnp.where(sh.low, roll(first, 64), second)
    whole = jnp.concatenate([stage[j, 0 : 3 * ROWS, :] for j in range(4)] + [stage[4, 0 : 3 * ROWS, 0:64]], axis=1)
    parts = jnp.concatenate(pieces(whole, 2), axis=0)
    moved = lax.dot_general(parts, perm[...], (((1,), (1,)), ((), ())), preferred_element_type=F32)
    moved = moved[3 * ROWS :] + moved[: 3 * ROWS]
    for c in range(3):
        states_ref[:, c, :, :] = moved[c * ROWS : (c + 1) * ROWS].reshape(EZ, VOX, YZ)


def micro(phases, grain, phase_cond, counts, current, load):
    smem = pl.BlockSpec(memory_space=pltpu.SMEM)
    vmem = pl.BlockSpec(memory_space=pltpu.VMEM)
    field = pltpu.VMEM((3 * CELLS, 8, 128), F32)
    return pl.pallas_call(
        micro_kernel,
        out_shape=(
            jax.ShapeDtypeStruct((EZ, 3, VOX, YZ), F32),
            jax.ShapeDtypeStruct((EZ, 3, 3), F32),
            jax.ShapeDtypeStruct((1, 128), F32),
        ),
        in_specs=[smem, smem, smem, smem, vmem, vmem],
        out_specs=(vmem, vmem, vmem),
        scratch_shapes=[
            pltpu.VMEM((YZ, YZ), BF16),
            pltpu.VMEM((5, 3 * ROWS, 128), F32),
            field, field, field, field, field, field,
            pltpu.VMEM((3 * PLANE, 8, 128), F32),
        ],
        compiler_params=pltpu.CompilerParams(vmem_limit_bytes=60 * 1024 * 1024),
        name="micro",
    )(phase_cond, counts, current, load, phases, grain)


def coarse_kernel(packed_ref, increment_ref, residual_ref, grid, send_a, recv_a, send_b, recv_b):
    rows, cols = 8, 32
    i, j = lax.axis_index("row"), lax.axis_index("col")
    barrier = pltpu.get_barrier_semaphore()

    def greet_col(s, _):
        pl.semaphore_signal(barrier, inc=1, device_id=(i, lax.rem(j + s, cols)), device_id_type=MESH)
        return 0

    def greet_row(s, _):
        pl.semaphore_signal(barrier, inc=1, device_id=(lax.rem(i + s, rows), j), device_id_type=MESH)
        return 0

    lax.fori_loop(1, cols, greet_col, 0)
    lax.fori_loop(1, rows, greet_row, 0)
    pl.semaphore_wait(barrier, cols + rows - 2)

    def along_col(s):
        return pltpu.make_async_remote_copy(
            src_ref=packed_ref,
            dst_ref=grid.at[i, pl.ds(j, 1)],
            send_sem=send_a.at[s],
            recv_sem=recv_a.at[s],
            device_id=(i, lax.rem(j + s, cols)),
            device_id_type=MESH,
        )

    def along_row(s):
        return pltpu.make_async_remote_copy(
            src_ref=grid.at[i],
            dst_ref=grid.at[i],
            send_sem=send_b.at[s],
            recv_sem=recv_b.at[s],
            device_id=(lax.rem(i + s, rows), j),
            device_id_type=MESH,
        )

    def start_col(s, _):
        along_col(s).start()
        return 0

    def wait_col(s, _):
        along_col(s).wait()
        return 0

    def start_row(s, _):
        along_row(s).start()
        return 0

    def wait_row(s, _):
        along_row(s).wait()
        return 0

    lax.fori_loop(1, cols, start_col, 0)
    grid[i, pl.ds(j, 1), :] = packed_ref[...]
    lax.fori_loop(1, cols, wait_col, 0)
    lax.fori_loop(1, rows, start_row, 0)
    lax.fori_loop(1, rows, wait_row, 0)

    lane = lane_iota()
    slot = lane >> 3
    sub = lax.broadcasted_iota(jnp.int32, (8, 128), 0)
    fields = [[jnp.zeros((8, 128), F32)] * 2 for _ in range(5)]
    for col in range(cols):
        at_col = grid[:, col, :]
        half, place = divmod(col, 16)
        for f in range(5):
            spun = roll(at_col, (place - f) * 8)
            fields[f][half] = jnp.where(slot == place, spun, fields[f][half])
    kx, ky, kz, current, load = fields

    def ahead_y(v):
        spun = [roll(part, -8) for part in v]
        return [jnp.where(slot == 15, spun[1], spun[0]), spun[1]]

    def back_y(v):
        spun = [roll(part, 8) for part in v]
        return [spun[0], jnp.where(slot == 0, spun[0], spun[1])]

    def ahead_z(v):
        return [roll(part, -1) for part in v]

    def back_z(v):
        return [roll(part, 1) for part in v]

    def ahead_x(v):
        return [pltpu.roll(part, 7, 0) for part in v]

    def back_x(v):
        return [pltpu.roll(part, 1, 0) for part in v]

    k_in = lane & 7
    never = lane < 0
    outside = [
        ([sub == 7] * 2, [sub == 0] * 2),
        ([never, slot == 15], [slot == 0, never]),
        ([k_in == 7] * 2, [k_in == 0] * 2),
    ]
    moves = [(ahead_x, back_x), (ahead_y, back_y), (ahead_z, back_z)]
    weights = []
    centre = [jnp.zeros((8, 128), F32)] * 2
    for (pair, masks), k in zip(zip(moves, outside), (kx, ky, kz)):
        for move, mask in zip(pair, masks):
            near = move(k)
            cond = [0.5 * (k[h] + jnp.where(mask[h], 0.0, near[h])) for h in range(2)]
            centre = [centre[h] + cond[h] for h in range(2)]
            weights.append((move, [jnp.where(mask[h], 0.0, cond[h]) for h in range(2)]))

    def apply(v):
        out = [centre[h] * v[h] for h in range(2)]
        for move, weight in weights:
            near = move(v)
            out = [out[h] - weight[h] * near[h] for h in range(2)]
        return out

    def dot(a, b):
        both = a[0] * b[0] + a[1] * b[1]
        both = jnp.sum(both, axis=0, keepdims=True)
        return jnp.broadcast_to(jnp.sum(both, axis=1, keepdims=True), (8, 128))

    image = apply(current)
    residual = [load[h] - image[h] for h in range(2)]
    increment = [jnp.zeros((8, 128), F32)] * 2
    direction = residual
    norm = dot(residual, residual)
    for _ in range(MACRO_ITERS):
        image = apply(direction)
        step = norm / dot(direction, image)
        increment = [increment[h] + step * direction[h] for h in range(2)]
        residual = [residual[h] - step * image[h] for h in range(2)]
        fresh = dot(residual, residual)
        ratio = fresh / norm
        direction = [residual[h] + ratio * direction[h] for h in range(2)]
        norm = fresh

    place = lax.rem(j, 16)

    def own(v):
        part = jnp.where(j < 16, v[0], v[1])
        part = jnp.where((sub == i) & (slot == place), part, 0.0)
        part = jnp.broadcast_to(jnp.sum(part, axis=0, keepdims=True), (8, 128))
        spun = pltpu.roll(part, lax.rem(128 - place * 8, 128), 1)
        return spun[0:1, 0:EZ]

    increment_ref[...] = own(increment)
    residual_ref[...] = own(residual)


def coarse(packed):
    vmem = pl.BlockSpec(memory_space=pltpu.VMEM)
    out = jax.ShapeDtypeStruct((1, EZ), F32)
    return pl.pallas_call(
        coarse_kernel,
        out_shape=(out, out),
        in_specs=[vmem],
        out_specs=(vmem, vmem),
        scratch_shapes=[
            pltpu.VMEM((8, 32, 128), F32),
            pltpu.SemaphoreType.DMA((32,)),
            pltpu.SemaphoreType.DMA((32,)),
            pltpu.SemaphoreType.DMA((8,)),
            pltpu.SemaphoreType.DMA((8,)),
        ],
        compiler_params=pltpu.CompilerParams(collective_id=0, has_side_effects=True),
        name="coarse",
    )(packed)


def shards(phases, grain, phase_cond, micro_counts, current, load):
    states, tangent, packed = micro(
        phases.reshape(EZ, VOX, YZ), grain.reshape(EZ, VOX, YZ), phase_cond,
        micro_counts.reshape(EZ), current.reshape(EZ), load.reshape(EZ),
    )
    increment, residual = coarse(packed)
    return (
        states.reshape(1, 1, EZ, 3, VOX, YZ),
        tangent.reshape(1, 1, EZ, 3, 3),
        increment.reshape(1, 1, EZ),
        residual.reshape(1, 1, EZ),
    )


def solution(mesh):
    in_specs = (
        P("row", "col", None, None, None),
        P("row", "col", None, None, None),
        P(),
        P("row", "col", None),
        P("row", "col", None),
        P("row", "col", None),
    )
    out_specs = (
        P("row", "col", None, None, None, None),
        P("row", "col", None, None, None),
        P("row", "col", None),
        P("row", "col", None),
    )
    return jax.shard_map(shards, mesh=mesh, in_specs=in_specs, out_specs=out_specs, check_vma=False)
```

time: 328 us -> 73.9 us (0.23)
  blocking collectives: 137 us -> 0 us
  Pallas kernels: 0 us -> 69.3 us
  other arithmetic: 67.7 us -> 0 us
  loops' own time: 48.6 us -> 0 us
  local copies, waits for them, and re-layouts: 52.2 us -> 3.71 us
  between operations: 21 us -> 0.64 us
    all_gather x4 -> x0, blocking collectives: 137 us -> none  [gather_in_order(): pieces = lax.all_gather(pieces, axes[k])]
    pallas_call x0 -> x2, Pallas kernels: none -> 69.3 us  [the longest x1 44.7 us: micro(): pl.pallas_call(micro_kernel, out_shape=(jax.ShapeDtypeStruct((EZ, 3, VOX,...]
    reduce_sum x145 -> x0, other arithmetic: 50.7 us -> none  [the longest x57 24.1 us: sweep(): step_size = norm_now / jnp.sum(direction * image, axis=(1, 2))]
    another operation x9 -> x0, loops' own time: 48.6 us -> none  [the longest x8 46.5 us: solve_rve(): fluct = lax.fori_loop(0, count, sweep, start)[0]]
    slice x611 -> x0, local copies, waits for them, and re-layouts: 41.1 us -> none  [the longest x130 11.7 us: forward(): return jnp.roll(field, -VOX, axis=-1)]
    add x63 -> x0, other arithmetic: 7.46 us -> none  [the longest x57 7.41 us: sweep(): direction = remain + (norm_next / norm_now)[:, None, None] * direction]
    dynamic_slice x8 -> x0, local copies, waits for them, and re-layouts: 4.71 us -> none  [solve_batch(): return lax.map(lambda pair: solve_rve(pair[0], pair[1]), (conduct, counts))]
where the time goes in v1:
time: 73.9 us; the launch traced here: 73.7 us
  Pallas kernels  69.3 us (94%)
  local copies, waits for them, and re-layouts  3.71 us (5%)
    pallas_call x1, Pallas kernels, micro(): pl.pallas_call(micro_kernel, out_shape=(jax.ShapeDtypeStruct((EZ, 3, VOX,...  44.7 us
    pallas_call x1, Pallas kernels, coarse(): pl.pallas_call(coarse_kernel, out_shape=(out, out), in_specs=[vmem], out_...  24.6 us
    unnamed x3, local copies, waits for them, and re-layouts  3.71 us

profile of v1, /device:TPU:1, one launch (start us, length us, event | category | flops | bytes accessed | tf_op | source)
XLA Modules:
  0.0 73.7 jit_solution(8295488932684076787)
XLA Ops:
  0.6 44.7 %micro.1 = (f32[8,3,24,576]{3,2,1,0:T(8,128)}, f32[8,3,3]{2,1,0:T(4,128)}, f32[1,128]{1,0:T(1,128)}) custom-call(f32[3]{0:T(128)} %cond_ref.1, s32[8]{0:T(128)} %bitcast.12, f32[8]{0:T(128)} %bitcast.13, f32[8]{0:T(128)} %bitcast.14, s32[8,24,576]{2,1,0:T(8,128)} %bitcast.9, f32[8,24,576]{2,1,0:T(8,128)} %bitcast.10), custom_call_target="tpu_custom_call" | custom-call | tf_op jit(solution)/shard_map/micro/pallas_call | solution.py:265
  45.4 1.4 %copy.11 = f32[1,1,8,3,3]{2,1,4,3,0:T(1,128)} copy(f32[1,1,8,3,3]{4,3,2,1,0:T(4,128)} %bitcast.11) | data formatting | bytes 576
  46.8 24.6 %coarse.1 = (f32[1,8]{1,0:T(1,128)}, f32[1,8]{1,0:T(1,128)}) custom-call(f32[1,128]{1,0:T(1,128)} %get-tuple-element.11.packed_ref), custom_call_target="tpu_custom_call" | custom-call | tf_op jit(solution)/shard_map/coarse/pallas_call | solution.py:436
  71.4 1.1 %copy.16 = f32[1,1,8]{2,1,0:T(1,128)} copy(f32[1,1,8]{2,1,0:T(1,128)} %bitcast.17) | data formatting | bytes 64
  72.5 1.2 %copy.17 = f32[1,1,8]{2,1,0:T(1,128)} copy(f32[1,1,8]{2,1,0:T(1,128)} %bitcast.16) | data formatting | bytes 64

commit v2 on v1

--- a/solution.py
+++ b/solution.py
@@ -17,6 +17,8 @@
 PLANE = 9
 CELLS = NX * PLANE
 ROWS = EZ * VOX
+HALO = 162
+CHUNK = 12
 F32 = jnp.float32
 BF16 = jnp.bfloat16
 MESH = pl.DeviceIdType.MESH
@@ -35,24 +37,17 @@
         lane = lane_iota()
         ys = (lane >> 3) & 7
         zs = lane & 7
-        self.y_last, self.y_first = ys == 7, ys == 0
-        self.z_last, self.z_first = zs == 7, zs == 0
+        self.y_up = self.gather(jnp.where(ys == 7, lane - 56, lane + 8))
+        self.y_down = self.gather(jnp.where(ys == 0, lane + 56, lane - 8))
+        self.z_up = self.gather(jnp.where(zs == 7, lane - 7, lane + 1))
+        self.z_down = self.gather(jnp.where(zs == 0, lane + 7, lane - 1))
         self.low = lane < 64
+
+    def gather(self, source):
+        return lambda v: jnp.take_along_axis(v, source, axis=1, mode="promise_in_bounds")
 
     def x_swap(self, v):
         return roll(v, 64)
-
-    def y_up(self, v):
-        return jnp.where(self.y_last, roll(v, 56), roll(v, -8))
-
-    def y_down(self, v):
-        return jnp.where(self.y_first, roll(v, -56), roll(v, 8))
-
-    def z_up(self, v):
-        return jnp.where(self.z_last, roll(v, 7), roll(v, -1))
-
-    def z_down(self, v):
-        return jnp.where(self.z_first, roll(v, -7), roll(v, 1))
 
 
 def pieces(v, count):
@@ -82,7 +77,7 @@
 def micro_kernel(
     cond_ref, counts_ref, current_ref, load_ref, phases_ref, grain_ref,
     states_ref, tangent_ref, packed_ref,
-    perm, stage, face, rhs, fluct, remain, direct, image, edge,
+    perm, stage, face, low_face, rhs, fluct, remain, direct, image, halo,
 ):
     sh = Shifts()
     cells = [(x, y, z) for x in range(NX) for y in range(3) for z in range(3)]
@@ -111,15 +106,31 @@
             if j < 4:
                 image[x * PLANE + 2 * j + 1] = jnp.where(sh.low, roll(low, 64), high)
 
+    for x in range(NX):
+        for z in range(3):
+            halo[x * 3 + z] = sh.y_up(image[at(x, 0, z)])
+    for x in range(NX):
+        for y in range(3):
+            halo[36 + x * 3 + y] = sh.z_up(image[at(x, y, 0)])
+    for k in range(PLANE):
+        halo[144 + k] = sh.x_swap(image[k])
     for x, y, z in cells:
         t = at(x, y, z)
         here = image[t]
-        ahead = image[t + PLANE] if x < NX - 1 else sh.x_swap(image[at(0, y, z)])
+        ahead = image[t + PLANE] if x < NX - 1 else halo[144 + y * 3 + z]
         face[t] = (here + ahead) * 0.5
-        ahead = image[t + 3] if y < 2 else sh.y_up(image[at(x, 0, z)])
+        ahead = image[t + 3] if y < 2 else halo[x * 3 + z]
         face[CELLS + t] = (here + ahead) * 0.5
-        ahead = image[t + 1] if z < 2 else sh.z_up(image[at(x, y, 0)])
+        ahead = image[t + 1] if z < 2 else halo[36 + x * 3 + y]
         face[2 * CELLS + t] = (here + ahead) * 0.5
+    for x in range(NX):
+        for z in range(3):
+            low_face[x * 3 + z] = sh.y_down(face[CELLS + at(x, 2, z)])
+    for x in range(NX):
+        for y in range(3):
+            low_face[36 + x * 3 + y] = sh.z_down(face[2 * CELLS + at(x, y, 2)])
+    for k in range(PLANE):
+        low_face[72 + k] = sh.x_swap(face[at(NX - 1, 0, 0) + k])
 
     zero = jnp.zeros((8, 128), F32)
     norms = [zero] * 3
@@ -127,9 +138,9 @@
     for x, y, z in cells:
         t = at(x, y, z)
         back = [
-            face[t - PLANE] if x > 0 else sh.x_swap(face[at(NX - 1, y, z)]),
-            face[CELLS + t - 3] if y > 0 else sh.y_down(face[CELLS + at(x, 2, z)]),
-            face[2 * CELLS + t - 1] if z > 0 else sh.z_down(face[2 * CELLS + at(x, y, 2)]),
+            face[t - PLANE] if x > 0 else low_face[72 + y * 3 + z],
+            face[CELLS + t - 3] if y > 0 else low_face[x * 3 + z],
+            face[2 * CELLS + t - 1] if z > 0 else low_face[36 + x * 3 + y],
         ]
         for c in range(3):
             here = face[c * CELLS + t]
@@ -146,81 +157,117 @@
     for k in range(EZ):
         counts = jnp.where(sub == k, counts_ref[k], counts)
 
-    def sweep(index, carry):
-        norm, alpha, beta = carry
-        new_alpha, new_norm, new_beta = [], [], []
-        for c in range(3):
-            base = c * CELLS
-
-            def renew(x):
-                plane = {}
+    def update(c, alpha, beta):
+        base, edge = c * CELLS, c * HALO
+        for first in range(0, NX, CHUNK):
+            span = range(first, first + CHUNK)
+            plane = {}
+            for x in span:
+                for k in range(PLANE):
+                    t = base + x * PLANE + k
+                    old = direct[t]
+                    fluct[t] = fluct[t] + alpha * old
+                    plane[x, k] = remain[t] + beta * old
+                    direct[t] = plane[x, k]
+                yield
+            for x in span:
+                for z in range(3):
+                    halo[edge + x * 3 + z] = sh.y_up(plane[x, z])
+            for x in span:
+                for z in range(3):
+                    halo[edge + 72 + x * 3 + z] = sh.y_down(plane[x, 6 + z])
+            for x in span:
                 for y in range(3):
-                    for z in range(3):
-                        t = base + at(x, y, z)
-                        old = direct[t]
-                        fluct[t] = fluct[t] + alpha[c] * old
-                        plane[y, z] = remain[t] + beta[c] * old
-                        direct[t] = plane[y, z]
-                return plane
-
-            last = renew(NX - 1)
-            here = renew(0)
-            before = {}
+                    halo[edge + 36 + x * 3 + y] = sh.z_up(plane[x, 3 * y])
+            for x in span:
+                for y in range(3):
+                    halo[edge + 108 + x * 3 + y] = sh.z_down(plane[x, 3 * y + 2])
+            if first == 0:
+                for k in range(PLANE):
+                    halo[edge + 144 + k] = sh.x_swap(plane[0, k])
+            if first + CHUNK == NX:
+                for k in range(PLANE):
+                    halo[edge + 153 + k] = sh.x_swap(plane[NX - 1, k])
+
+    def stencil(c, box):
+        base, edge = c * CELLS, c * HALO
+        acc = zero
+        here = [direct[base + k] for k in range(PLANE)]
+        before = [low_face[72 + k] * (halo[edge + 153 + k] - here[k]) for k in range(PLANE)]
+        for x in range(NX):
+            if x < NX - 1:
+                ahead = [direct[base + (x + 1) * PLANE + k] for k in range(PLANE)]
+            else:
+                ahead = [halo[edge + 144 + k] for k in range(PLANE)]
             for y in range(3):
+                if y == 0:
+                    flux_y = [low_face[x * 3 + z] * (halo[edge + 72 + x * 3 + z] - here[z]) for z in range(3)]
+                flux_z = low_face[36 + x * 3 + y] * (halo[edge + 108 + x * 3 + y] - here[3 * y])
                 for z in range(3):
-                    flux = face[at(NX - 1, y, z)] * (last[y, z] - sh.x_swap(here[y, z]))
-                    edge[c * PLANE + y * 3 + z] = flux
-                    before[y, z] = sh.x_swap(flux)
-            acc = zero
-            for x in range(NX):
-                if x < NX - 2:
-                    ahead = renew(x + 1)
-                elif x == NX - 2:
-                    ahead = {(y, z): direct[base + at(x + 1, y, z)] for y in range(3) for z in range(3)}
-                flux_x, flux_y, flux_z = {}, {}, {}
-                for y in range(3):
-                    for z in range(3):
-                        t = at(x, y, z)
-                        v = here[y, z]
-                        if x < NX - 1:
-                            flux_x[y, z] = face[t] * (v - ahead[y, z])
-                        else:
-                            flux_x[y, z] = edge[c * PLANE + y * 3 + z]
-                        up = here[y + 1, z] if y < 2 else sh.y_up(here[0, z])
-                        flux_y[y, z] = face[CELLS + t] * (v - up)
-                        up = here[y, z + 1] if z < 2 else sh.z_up(here[y, 0])
-                        flux_z[y, z] = face[2 * CELLS + t] * (v - up)
-                for y in range(3):
-                    for z in range(3):
-                        t = base + at(x, y, z)
-                        down_y = flux_y[y - 1, z] if y > 0 else sh.y_down(flux_y[2, z])
-                        down_z = flux_z[y, z - 1] if z > 0 else sh.z_down(flux_z[y, 2])
-                        out = (flux_x[y, z] - before[y, z]) + ((flux_y[y, z] - down_y) + (flux_z[y, z] - down_z))
-                        image[t] = out
-                        acc = acc + here[y, z] * out
-                before, here = flux_x, ahead
-            step = norm[c] / total(acc)
-            new_alpha.append(jnp.where(index < counts, step, 0.0))
-        for c in range(3):
-            base = c * CELLS
-            acc = zero
-            for t in range(base, base + CELLS):
-                value = remain[t] - new_alpha[c] * image[t]
+                    k = 3 * y + z
+                    t = x * PLANE + k
+                    v = here[k]
+                    next_x = face[t] * (v - ahead[k])
+                    up = here[k + 3] if y < 2 else halo[edge + x * 3 + z]
+                    next_y = face[CELLS + t] * (v - up)
+                    up = here[k + 1] if z < 2 else halo[edge + 36 + x * 3 + y]
+                    next_z = face[2 * CELLS + t] * (v - up)
+                    out = (next_x - before[k]) + ((next_y - flux_y[z]) + (next_z - flux_z))
+                    image[base + t] = out
+                    acc = acc + v * out
+                    before[k], flux_y[z], flux_z = next_x, next_y, next_z
+            here = ahead
+            yield
+        box.append(acc)
+
+    def descend(c, alpha, box):
+        acc = zero
+        for x in range(NX):
+            for t in range(c * CELLS + x * PLANE, c * CELLS + (x + 1) * PLANE):
+                value = remain[t] - alpha * image[t]
                 remain[t] = value
                 acc = acc + value * value
-            fresh = total(acc)
-            new_norm.append(fresh)
-            new_beta.append(fresh / norm[c])
-        return tuple(new_norm), tuple(new_alpha), tuple(new_beta)
+            yield
+        box.append(acc)
+
+    def together(*parts):
+        parts = list(parts)
+        while parts:
+            for part in list(parts):
+                if next(part, part) is part:
+                    parts.remove(part)
+
+    def sweep(index, carry):
+        norm, alpha, beta, last = carry
+        live = index < counts
+        box = []
+        together(stencil(0, box), update(1, alpha[1], beta[1]))
+        step_0 = jnp.where(live, norm[0] / total(box[0]), 0.0)
+        norm_2 = total(last)
+        together(stencil(1, box), update(2, alpha[2], norm_2 / norm[2]))
+        step_1 = jnp.where(live, norm[1] / total(box[1]), 0.0)
+        together(stencil(2, box), descend(0, step_0, box))
+        acc_2, acc_0 = (box[2], box[3])
+        step_2 = jnp.where(live, norm_2 / total(acc_2), 0.0)
+        norm_0 = total(acc_0)
+        together(descend(1, step_1, box))
+        norm_1 = total(box[4])
+        together(descend(2, step_2, box))
+        together(update(0, step_0, norm_0 / norm[0]))
+        return (norm_0, norm_1, norm_2), (step_0, step_1, step_2), (zero, norm_1 / norm[1]), box[5]
 
     norm = tuple(total(v) for v in norms)
-    norm, alpha, beta = lax.fori_loop(0, MICRO_MAX, sweep, (norm, (zero,) * 3, (zero,) * 3))
+    together(update(0, zero, zero))
+    first = (norm, (zero,) * 3, (zero, zero), jnp.where(lane_iota() == 0, norm[2], 0.0))
+    norm, alpha, _, _ = lax.fori_loop(0, MICRO_MAX, sweep, first)
 
     inner = [[zero] * 3 for _ in range(3)]
     for t in range(CELLS):
         for c in range(3):
-            value = fluct[c * CELLS + t] + alpha[c] * direct[c * CELLS + t]
-            fluct[c * CELLS + t] = value
+            value = fluct[c * CELLS + t]
+            if c > 0:
+                value = value + alpha[c] * direct[c * CELLS + t]
+                fluct[c * CELLS + t] = value
             for d in range(3):
                 inner[d][c] = inner[d][c] + value * rhs[d * CELLS + t]
     scale = 1.0 / (VOX * YZ)
@@ -274,8 +321,10 @@
         scratch_shapes=[
             pltpu.VMEM((YZ, YZ), BF16),
             pltpu.VMEM((5, 3 * ROWS, 128), F32),
-            field, field, field, field, field, field,
-            pltpu.VMEM((3 * PLANE, 8, 128), F32),
+            field,
+            pltpu.VMEM((81, 8, 128), F32),
+            field, field, field, field, field,
+            pltpu.VMEM((3 * HALO, 8, 128), F32),
         ],
         compiler_params=pltpu.CompilerParams(vmem_limit_bytes=60 * 1024 * 1024),
         name="micro",

time: 73.9 us -> 53.7 us (0.73)
  Pallas kernels: 69.3 us -> 49.2 us
    pallas_call x1, Pallas kernels: 44.7 us -> 24.6 us  [micro(): pl.pallas_call(micro_kernel, out_shape=(jax.ShapeDtypeStruct((EZ, 3, VOX,...]
where the time goes in v2:
time: 53.7 us; the launch traced here: 53.5 us
  Pallas kernels  49.2 us (92%)
  local copies, waits for them, and re-layouts  3.71 us (7%)
  between operations  0.64 us (1%)
    pallas_call x1, Pallas kernels, coarse(): pl.pallas_call(coarse_kernel, out_shape=(out, out), in_specs=[vmem], out_...  24.6 us
    pallas_call x1, Pallas kernels, micro(): pl.pallas_call(micro_kernel, out_shape=(jax.ShapeDtypeStruct((EZ, 3, VOX,...  24.6 us
    unnamed x3, local copies, waits for them, and re-layouts  3.71 us

profile of v2, /device:TPU:1, one launch (start us, length us, event | category | flops | bytes accessed | tf_op | source)
XLA Modules:
  0.0 53.5 jit_solution(15668235117494145157)
XLA Ops:
  0.6 24.6 %micro.1 = (f32[8,3,24,576]{3,2,1,0:T(8,128)}, f32[8,3,3]{2,1,0:T(4,128)}, f32[1,128]{1,0:T(1,128)}) custom-call(f32[3]{0:T(128)} %cond_ref.1, s32[8]{0:T(128)} %bitcast.12, f32[8]{0:T(128)} %bitcast.13, f32[8]{0:T(128)} %bitcast.14, s32[8,24,576]{2,1,0:T(8,128)} %bitcast.9, f32[8,24,576]{2,1,0:T(8,128)} %bitcast.10), custom_call_target="tpu_custom_call" | custom-call | tf_op jit(solution)/shard_map/micro/pallas_call | solution.py:312
  25.2 1.4 %copy.11 = f32[1,1,8,3,3]{2,1,4,3,0:T(1,128)} copy(f32[1,1,8,3,3]{4,3,2,1,0:T(4,128)} %bitcast.11) | data formatting | bytes 576
  26.6 24.6 %coarse.1 = (f32[1,8]{1,0:T(1,128)}, f32[1,8]{1,0:T(1,128)}) custom-call(f32[1,128]{1,0:T(1,128)} %get-tuple-element.11.packed_ref), custom_call_target="tpu_custom_call" | custom-call | tf_op jit(solution)/shard_map/coarse/pallas_call | solution.py:485
  51.2 1.1 %copy.16 = f32[1,1,8]{2,1,0:T(1,128)} copy(f32[1,1,8]{2,1,0:T(1,128)} %bitcast.17) | data formatting | bytes 64
  52.3 1.2 %copy.17 = f32[1,1,8]{2,1,0:T(1,128)} copy(f32[1,1,8]{2,1,0:T(1,128)} %bitcast.16) | data formatting | bytes 64

commit v3 on v2

--- a/solution.py
+++ b/solution.py
@@ -74,11 +74,27 @@
     return jnp.broadcast_to(jnp.sum(v, axis=1, keepdims=True), (8, 128))
 
 
-def micro_kernel(
+def heavy_kernel(
     cond_ref, counts_ref, current_ref, load_ref, phases_ref, grain_ref,
-    states_ref, tangent_ref, packed_ref,
-    perm, stage, face, low_face, rhs, fluct, remain, direct, image, halo,
+    states_ref, tangent_ref, grid_ref,
+    perm, stage, face, low_face, rhs, fluct, remain, direct, image, halo, packed, states,
+    send_a, recv_a, send_b, recv_b, out_sem,
 ):
+    rows, cols = 8, 32
+    row_at, col_at = lax.axis_index("row"), lax.axis_index("col")
+    barrier = pltpu.get_barrier_semaphore()
+
+    def greet_col(s, _):
+        pl.semaphore_signal(barrier, inc=1, device_id=(row_at, lax.rem(col_at + s, cols)), device_id_type=MESH)
+        return 0
+
+    def greet_row(s, _):
+        pl.semaphore_signal(barrier, inc=1, device_id=(lax.rem(row_at + s, rows), col_at), device_id_type=MESH)
+        return 0
+
+    lax.fori_loop(1, cols, greet_col, 0)
+    lax.fori_loop(1, rows, greet_row, 0)
+
     sh = Shifts()
     cells = [(x, y, z) for x in range(NX) for y in range(3) for z in range(3)]
 
@@ -277,8 +293,9 @@
     ]
     lane = lane_iota()
     for d in range(3):
-        rows = jnp.where(lane == 0, tangent[d][0], jnp.where(lane == 1, tangent[d][1], tangent[d][2]))
-        tangent_ref[:, d, :] = rows[:, 0:3]
+        for c in range(3):
+            spread = jnp.sum(jnp.where(sub == (lane & 7), tangent[d][c], 0.0), axis=0, keepdims=True)
+            tangent_ref[d, c] = spread[:, 0:EZ]
 
     slot = lane >> 3
     message = jnp.where(slot == 0, tangent[0][0], jnp.where(slot == 1, tangent[1][1], tangent[2][2]))
@@ -288,7 +305,47 @@
     for k in range(EZ):
         message = jnp.where(low == 24 + k, current_ref[k], message)
         message = jnp.where(low == 32 + k, load_ref[k], message)
-    packed_ref[...] = message
+    packed[...] = message
+    pl.semaphore_wait(barrier, cols + rows - 2)
+
+    def along_col(s):
+        return pltpu.make_async_remote_copy(
+            src_ref=packed,
+            dst_ref=grid_ref.at[row_at, pl.ds(col_at, 1)],
+            send_sem=send_a.at[s],
+            recv_sem=recv_a.at[s],
+            device_id=(row_at, lax.rem(col_at + s, cols)),
+            device_id_type=MESH,
+        )
+
+    def along_row(s):
+        return pltpu.make_async_remote_copy(
+            src_ref=grid_ref.at[row_at],
+            dst_ref=grid_ref.at[row_at],
+            send_sem=send_b.at[s],
+            recv_sem=recv_b.at[s],
+            device_id=(lax.rem(row_at + s, rows), col_at),
+            device_id_type=MESH,
+        )
+
+    def start_col(s, _):
+        along_col(s).start()
+        return 0
+
+    def wait_col(s, _):
+        along_col(s).wait()
+        return 0
+
+    def start_row(s, _):
+        along_row(s).start()
+        return 0
+
+    def wait_row(s, _):
+        along_row(s).wait()
+        return 0
+
+    lax.fori_loop(1, cols, start_col, 0)
+    grid_ref[row_at, pl.ds(col_at, 1), :] = message
 
     for c in range(3):
         for x in range(NX):
@@ -302,22 +359,28 @@
     moved = lax.dot_general(parts, perm[...], (((1,), (1,)), ((), ())), preferred_element_type=F32)
     moved = moved[3 * ROWS :] + moved[: 3 * ROWS]
     for c in range(3):
-        states_ref[:, c, :, :] = moved[c * ROWS : (c + 1) * ROWS].reshape(EZ, VOX, YZ)
-
-
-def micro(phases, grain, phase_cond, counts, current, load):
+        states[:, c, :, :] = moved[c * ROWS : (c + 1) * ROWS].reshape(EZ, VOX, YZ)
+    out = pltpu.make_async_copy(states, states_ref, out_sem)
+    out.start()
+    lax.fori_loop(1, cols, wait_col, 0)
+    lax.fori_loop(1, rows, start_row, 0)
+    lax.fori_loop(1, rows, wait_row, 0)
+    out.wait()
+
+
+def heavy(phases, grain, phase_cond, counts, current, load):
     smem = pl.BlockSpec(memory_space=pltpu.SMEM)
     vmem = pl.BlockSpec(memory_space=pltpu.VMEM)
     field = pltpu.VMEM((3 * CELLS, 8, 128), F32)
     return pl.pallas_call(
-        micro_kernel,
+        heavy_kernel,
         out_shape=(
             jax.ShapeDtypeStruct((EZ, 3, VOX, YZ), F32),
-            jax.ShapeDtypeStruct((EZ, 3, 3), F32),
-            jax.ShapeDtypeStruct((1, 128), F32),
+            jax.ShapeDtypeStruct((3, 3, 1, EZ), F32),
+            jax.ShapeDtypeStruct((8, 32, 128), F32),
         ),
         in_specs=[smem, smem, smem, smem, vmem, vmem],
-        out_specs=(vmem, vmem, vmem),
+        out_specs=(pl.BlockSpec(memory_space=pl.ANY), vmem, vmem),
         scratch_shapes=[
             pltpu.VMEM((YZ, YZ), BF16),
             pltpu.VMEM((5, 3 * ROWS, 128), F32),
@@ -325,70 +388,31 @@
             pltpu.VMEM((81, 8, 128), F32),
             field, field, field, field, field,
             pltpu.VMEM((3 * HALO, 8, 128), F32),
+            pltpu.VMEM((1, 128), F32),
+            pltpu.VMEM((EZ, 3, VOX, YZ), F32),
+            pltpu.SemaphoreType.DMA((32,)),
+            pltpu.SemaphoreType.DMA((32,)),
+            pltpu.SemaphoreType.DMA((8,)),
+            pltpu.SemaphoreType.DMA((8,)),
+            pltpu.SemaphoreType.DMA,
         ],
-        compiler_params=pltpu.CompilerParams(vmem_limit_bytes=60 * 1024 * 1024),
+        compiler_params=pltpu.CompilerParams(
+            vmem_limit_bytes=62 * 1024 * 1024, collective_id=0, has_side_effects=True
+        ),
         name="micro",
     )(phase_cond, counts, current, load, phases, grain)
 
 
-def coarse_kernel(packed_ref, increment_ref, residual_ref, grid, send_a, recv_a, send_b, recv_b):
-    rows, cols = 8, 32
+def coarse_kernel(
+    grid, states_in, tangent_in, states_ref, tangent_ref, increment_ref, residual_ref, states, in_sem, out_sem
+):
+    cols = 32
     i, j = lax.axis_index("row"), lax.axis_index("col")
-    barrier = pltpu.get_barrier_semaphore()
-
-    def greet_col(s, _):
-        pl.semaphore_signal(barrier, inc=1, device_id=(i, lax.rem(j + s, cols)), device_id_type=MESH)
-        return 0
-
-    def greet_row(s, _):
-        pl.semaphore_signal(barrier, inc=1, device_id=(lax.rem(i + s, rows), j), device_id_type=MESH)
-        return 0
-
-    lax.fori_loop(1, cols, greet_col, 0)
-    lax.fori_loop(1, rows, greet_row, 0)
-    pl.semaphore_wait(barrier, cols + rows - 2)
-
-    def along_col(s):
-        return pltpu.make_async_remote_copy(
-            src_ref=packed_ref,
-            dst_ref=grid.at[i, pl.ds(j, 1)],
-            send_sem=send_a.at[s],
-            recv_sem=recv_a.at[s],
-            device_id=(i, lax.rem(j + s, cols)),
-            device_id_type=MESH,
-        )
-
-    def along_row(s):
-        return pltpu.make_async_remote_copy(
-            src_ref=grid.at[i],
-            dst_ref=grid.at[i],
-            send_sem=send_b.at[s],
-            recv_sem=recv_b.at[s],
-            device_id=(lax.rem(i + s, rows), j),
-            device_id_type=MESH,
-        )
-
-    def start_col(s, _):
-        along_col(s).start()
-        return 0
-
-    def wait_col(s, _):
-        along_col(s).wait()
-        return 0
-
-    def start_row(s, _):
-        along_row(s).start()
-        return 0
-
-    def wait_row(s, _):
-        along_row(s).wait()
-        return 0
-
-    lax.fori_loop(1, cols, start_col, 0)
-    grid[i, pl.ds(j, 1), :] = packed_ref[...]
-    lax.fori_loop(1, cols, wait_col, 0)
-    lax.fori_loop(1, rows, start_row, 0)
-    lax.fori_loop(1, rows, wait_row, 0)
+    inward = [pltpu.make_async_copy(states_in.at[e], states.at[e], in_sem.at[e]) for e in range(EZ)]
+    outward = [pltpu.make_async_copy(states.at[e], states_ref.at[e], out_sem.at[e]) for e in range(EZ)]
+    for copy in inward:
+        copy.start()
+    tangent_ref[...] = tangent_in[...]
 
     lane = lane_iota()
     slot = lane >> 3
@@ -401,6 +425,9 @@
             spun = roll(at_col, (place - f) * 8)
             fields[f][half] = jnp.where(slot == place, spun, fields[f][half])
     kx, ky, kz, current, load = fields
+    for before, after in zip(inward, outward):
+        before.wait()
+        after.start()
 
     def ahead_y(v):
         spun = [roll(part, -8) for part in v]
@@ -477,37 +504,42 @@
 
     increment_ref[...] = own(increment)
     residual_ref[...] = own(residual)
-
-
-def coarse(packed):
+    for copy in outward:
+        copy.wait()
+
+
+def coarse(grid, states, tangent):
     vmem = pl.BlockSpec(memory_space=pltpu.VMEM)
+    hbm = pl.BlockSpec(memory_space=pl.ANY)
     out = jax.ShapeDtypeStruct((1, EZ), F32)
     return pl.pallas_call(
         coarse_kernel,
-        out_shape=(out, out),
-        in_specs=[vmem],
-        out_specs=(vmem, vmem),
+        out_shape=(
+            jax.ShapeDtypeStruct((EZ, 3, VOX, YZ), F32),
+            jax.ShapeDtypeStruct((3, 3, 1, EZ), F32),
+            out,
+            out,
+        ),
+        in_specs=[vmem, hbm, vmem],
+        out_specs=(hbm, vmem, vmem, vmem),
         scratch_shapes=[
-            pltpu.VMEM((8, 32, 128), F32),
-            pltpu.SemaphoreType.DMA((32,)),
-            pltpu.SemaphoreType.DMA((32,)),
-            pltpu.SemaphoreType.DMA((8,)),
-            pltpu.SemaphoreType.DMA((8,)),
+            pltpu.VMEM((EZ, 3, VOX, YZ), F32),
+            pltpu.SemaphoreType.DMA((EZ,)),
+            pltpu.SemaphoreType.DMA((EZ,)),
         ],
-        compiler_params=pltpu.CompilerParams(collective_id=0, has_side_effects=True),
         name="coarse",
-    )(packed)
+    )(grid, states, tangent)
 
 
 def shards(phases, grain, phase_cond, micro_counts, current, load):
-    states, tangent, packed = micro(
+    states, tangent, grid = heavy(
         phases.reshape(EZ, VOX, YZ), grain.reshape(EZ, VOX, YZ), phase_cond,
         micro_counts.reshape(EZ), current.reshape(EZ), load.reshape(EZ),
     )
-    increment, residual = coarse(packed)
+    states, tangent, increment, residual = coarse(grid, states, tangent)
     return (
         states.reshape(1, 1, EZ, 3, VOX, YZ),
-        tangent.reshape(1, 1, EZ, 3, 3),
+        jnp.moveaxis(tangent, 3, 0).reshape(1, 1, EZ, 3, 3),
         increment.reshape(1, 1, EZ),
         residual.reshape(1, 1, EZ),
     )

time: 53.7 us -> 48 us (0.89)
  local copies, waits for them, and re-layouts: 3.71 us -> 0 us
  Pallas kernels: 49.2 us -> 47.2 us
    unnamed x3 -> x0, local copies, waits for them, and re-layouts: 3.71 us -> none
    pallas_call x2, Pallas kernels: 49.2 us -> 47.2 us  [the longest x1 41.9 us: heavy(): pl.pallas_call(heavy_kernel, out_shape=(jax.ShapeDtypeStruct((EZ, 3, VOX,...]
where the time goes in v3:
time: 48 us; the launch traced here: 47.8 us
  Pallas kernels  47.2 us (98%)
  between operations  0.64 us (1%)
    pallas_call x1, Pallas kernels, heavy(): pl.pallas_call(heavy_kernel, out_shape=(jax.ShapeDtypeStruct((EZ, 3, VOX,...  41.9 us
    pallas_call x1, Pallas kernels, coarse(): pl.pallas_call(coarse_kernel, out_shape=(jax.ShapeDtypeStruct((EZ, 3, VOX...  5.25 us

profile of v3, /device:TPU:1, one launch (start us, length us, event | category | flops | bytes accessed | tf_op | source)
XLA Modules:
  0.0 47.8 jit_solution(5675898807778505640)
XLA Ops:
  0.6 41.9 %micro.1 = (f32[8,3,24,576]{3,2,1,0:T(8,128)}, f32[3,3,1,8]{3,2,1,0:T(1,128)}, f32[8,32,128]{2,1,0:T(8,128)}) custom-call(f32[3]{0:T(128)} %cond_ref.1, s32[8]{0:T(128)} %bitcast.15, f32[8]{0:T(128)} %bitcast.16, f32[8]{0:T(128)} %bitcast.17, s32[8,24,576]{2,1,0:T(8,128)} %bitcast.13, f32[8,24,576]{2,1,0:T(8,128)} %bitcast.14), custom_call_target="tpu_custom_call" | custom-call | tf_op jit(solution)/shard_map/micro/pallas_call | solution.py:375
  42.6 5.2 %coarse.1 = (f32[8,3,24,576]{3,2,1,0:T(8,128)}, f32[3,3,1,8]{3,2,1,0:T(1,128)}, f32[1,8]{1,0:T(1,128)}, f32[1,8]{1,0:T(1,128)}) custom-call(f32[8,32,128]{2,1,0:T(8,128)} %get-tuple-element.11.grid, f32[8,3,24,576]{3,2,1,0:T(8,128)} %get-tuple-element.12.states_in, f32[3,3,1,8]{3,2,1,0:T(1,128)} %get-tuple-element.13.tangent_in), custom_call_target="tpu_custom_call" | custom-call | tf_op jit(solution)/shard_map/coarse/pallas_call | solution.py:515

commit v4 on v3

--- a/solution.py
+++ b/solution.py
@@ -18,7 +18,7 @@
 CELLS = NX * PLANE
 ROWS = EZ * VOX
 HALO = 162
-CHUNK = 12
+CHUNK = 3
 F32 = jnp.float32
 BF16 = jnp.bfloat16
 MESH = pl.DeviceIdType.MESH
@@ -257,10 +257,10 @@
         norm, alpha, beta, last = carry
         live = index < counts
         box = []
-        together(stencil(0, box), update(1, alpha[1], beta[1]))
+        together(update(1, alpha[1], beta[1]), stencil(0, box))
         step_0 = jnp.where(live, norm[0] / total(box[0]), 0.0)
         norm_2 = total(last)
-        together(stencil(1, box), update(2, alpha[2], norm_2 / norm[2]))
+        together(update(2, alpha[2], norm_2 / norm[2]), stencil(1, box))
         step_1 = jnp.where(live, norm[1] / total(box[1]), 0.0)
         together(stencil(2, box), descend(0, step_0, box))
         acc_2, acc_0 = (box[2], box[3])
@@ -308,43 +308,41 @@
     packed[...] = message
     pl.semaphore_wait(barrier, cols + rows - 2)
 
-    def along_col(s):
+    x_at, z_at = col_at // 8, lax.rem(col_at, 8)
+    y_at, core_at = row_at // 2, lax.rem(row_at, 2)
+
+    def hops(steps, lengths):
+        return sum(min(step, length - step) for step, length in zip(steps, lengths))
+
+    def along_col(s, dx, dz):
         return pltpu.make_async_remote_copy(
             src_ref=packed,
             dst_ref=grid_ref.at[row_at, pl.ds(col_at, 1)],
             send_sem=send_a.at[s],
             recv_sem=recv_a.at[s],
-            device_id=(row_at, lax.rem(col_at + s, cols)),
+            device_id=(row_at, lax.rem(x_at + dx, 4) * 8 + lax.rem(z_at + dz, 8)),
             device_id_type=MESH,
         )
 
-    def along_row(s):
+    def along_row(s, dy, dc):
         return pltpu.make_async_remote_copy(
             src_ref=grid_ref.at[row_at],
             dst_ref=grid_ref.at[row_at],
             send_sem=send_b.at[s],
             recv_sem=recv_b.at[s],
-            device_id=(lax.rem(row_at + s, rows), col_at),
+            device_id=(lax.rem(y_at + dy, 4) * 2 + lax.rem(core_at + dc, 2), col_at),
             device_id_type=MESH,
         )
 
-    def start_col(s, _):
-        along_col(s).start()
-        return 0
-
-    def wait_col(s, _):
-        along_col(s).wait()
-        return 0
-
-    def start_row(s, _):
-        along_row(s).start()
-        return 0
-
-    def wait_row(s, _):
-        along_row(s).wait()
-        return 0
-
-    lax.fori_loop(1, cols, start_col, 0)
+    col_steps = [(dx, dz) for dx in range(4) for dz in range(8) if dx or dz]
+    col_steps.sort(key=lambda steps: -hops(steps, (4, 8)))
+    row_steps = [(dy, dc) for dy in range(4) for dc in range(2) if dy or dc]
+    row_steps.sort(key=lambda steps: -hops(steps, (4, 2)))
+    col_copies = [along_col(s, *steps) for s, steps in enumerate(col_steps)]
+    row_copies = [along_row(s, *steps) for s, steps in enumerate(row_steps)]
+
+    for copy in col_copies:
+        copy.start()
     grid_ref[row_at, pl.ds(col_at, 1), :] = message
 
     for c in range(3):
@@ -362,9 +360,14 @@
         states[:, c, :, :] = moved[c * ROWS : (c + 1) * ROWS].reshape(EZ, VOX, YZ)
     out = pltpu.make_async_copy(states, states_ref, out_sem)
     out.start()
-    lax.fori_loop(1, cols, wait_col, 0)
-    lax.fori_loop(1, rows, start_row, 0)
-    lax.fori_loop(1, rows, wait_row, 0)
+    for copy in col_copies:
+        copy.wait_recv()
+    for copy in row_copies:
+        copy.start()
+    for copy in col_copies:
+        copy.wait_send()
+    for copy in row_copies:
+        copy.wait()
     out.wait()
 
 
@@ -481,17 +484,22 @@
     image = apply(current)
     residual = [load[h] - image[h] for h in range(2)]
     increment = [jnp.zeros((8, 128), F32)] * 2
-    direction = residual
-    norm = dot(residual, residual)
-    for _ in range(MACRO_ITERS):
-        image = apply(direction)
-        step = norm / dot(direction, image)
+    applied = apply(residual)
+    norm, curve = dot(residual, residual), dot(residual, applied)
+    step = norm / curve
+    direction, image = residual, applied
+    for iteration in range(MACRO_ITERS):
         increment = [increment[h] + step * direction[h] for h in range(2)]
         residual = [residual[h] - step * image[h] for h in range(2)]
-        fresh = dot(residual, residual)
+        if iteration == MACRO_ITERS - 1:
+            break
+        applied = apply(residual)
+        fresh, curve = dot(residual, residual), dot(residual, applied)
         ratio = fresh / norm
+        step = fresh / (curve - ratio * (fresh / step))
+        norm = fresh
         direction = [residual[h] + ratio * direction[h] for h in range(2)]
-        norm = fresh
+        image = [applied[h] + ratio * image[h] for h in range(2)]
 
     place = lax.rem(j, 16)
 

time: 48 us -> 45.8 us (0.954)
  Pallas kernels: 47.2 us -> 45 us
    pallas_call x1, Pallas kernels: 41.9 us -> 40.3 us  [heavy(): pl.pallas_call(heavy_kernel, out_shape=(jax.ShapeDtypeStruct((EZ, 3, VOX,...]
    pallas_call x1, Pallas kernels: 5.25 us -> 4.65 us  [coarse(): pl.pallas_call(coarse_kernel, out_shape=(jax.ShapeDtypeStruct((EZ, 3, VOX...]
where the time goes in v4:
time: 45.8 us; the launch traced here: 45.6 us
  Pallas kernels  45 us (98%)
  between operations  0.64 us (1%)
    pallas_call x1, Pallas kernels, heavy(): pl.pallas_call(heavy_kernel, out_shape=(jax.ShapeDtypeStruct((EZ, 3, VOX,...  40.3 us
    pallas_call x1, Pallas kernels, coarse(): pl.pallas_call(coarse_kernel, out_shape=(jax.ShapeDtypeStruct((EZ, 3, VOX...  4.65 us

profile of v4, /device:TPU:1, one launch (start us, length us, event | category | flops | bytes accessed | tf_op | source)
XLA Modules:
  0.0 45.6 jit_solution(5500653677660090193)
XLA Ops:
  0.6 40.3 %micro.1 = (f32[8,3,24,576]{3,2,1,0:T(8,128)}, f32[3,3,1,8]{3,2,1,0:T(1,128)}, f32[8,32,128]{2,1,0:T(8,128)}) custom-call(f32[3]{0:T(128)} %cond_ref.1, s32[8]{0:T(128)} %bitcast.15, f32[8]{0:T(128)} %bitcast.16, f32[8]{0:T(128)} %bitcast.17, s32[8,24,576]{2,1,0:T(8,128)} %bitcast.13, f32[8,24,576]{2,1,0:T(8,128)} %bitcast.14), custom_call_target="tpu_custom_call" | custom-call | tf_op jit(solution)/shard_map/micro/pallas_call | solution.py:378
  41.0 4.7 %coarse.1 = (f32[8,3,24,576]{3,2,1,0:T(8,128)}, f32[3,3,1,8]{3,2,1,0:T(1,128)}, f32[1,8]{1,0:T(1,128)}, f32[1,8]{1,0:T(1,128)}) custom-call(f32[8,32,128]{2,1,0:T(8,128)} %get-tuple-element.11.grid, f32[8,3,24,576]{3,2,1,0:T(8,128)} %get-tuple-element.12.states_in, f32[3,3,1,8]{3,2,1,0:T(1,128)} %get-tuple-element.13.tangent_in), custom_call_target="tpu_custom_call" | custom-call | tf_op jit(solution)/shard_map/coarse/pallas_call | solution.py:523

commit v5 on v4

--- a/solution.py
+++ b/solution.py
@@ -74,12 +74,32 @@
     return jnp.broadcast_to(jnp.sum(v, axis=1, keepdims=True), (8, 128))
 
 
+def gathered_rows(inbox, slot, sub):
+    spans = [pltpu.roll(inbox[8 * q : 8 * q + 8, :], q % 2 * 64, 1, stride=8, stride_axis=0) for q in range(4)]
+    block = [jnp.zeros((8, 128), F32)] * 2
+    for f in range(5):
+        for h in range(2):
+            both = jnp.zeros((8, 128), F32)
+            for q in (0, 1):
+                both = both + jnp.where(slot == ((8 * q + sub + f) & 15), spans[2 * h + q], 0.0)
+            row = 2 * f + h
+            line = jnp.broadcast_to(jnp.sum(both, axis=0, keepdims=True), (8, 128))
+            block[row // 8] = jnp.where(sub == row % 8, line, block[row // 8])
+    return jnp.concatenate(block, axis=0)
+
+
 def heavy_kernel(
-    cond_ref, counts_ref, current_ref, load_ref, phases_ref, grain_ref,
+    cond_ref, counts_ref, current_ref, load_ref, phases_in, grain_in,
     states_ref, tangent_ref, grid_ref,
-    perm, stage, face, low_face, rhs, fluct, remain, direct, image, halo, packed, states,
-    send_a, recv_a, send_b, recv_b, out_sem,
+    perm, stage, face, low_face, rhs, fluct, remain, direct, image, halo, packed, inbox, states, phases_ref, grain_ref,
+    send_a, recv_a, send_b, recv_b, out_sem, phases_sem, grain_sem,
 ):
+    inputs = [
+        pltpu.make_async_copy(phases_in, phases_ref, phases_sem),
+        pltpu.make_async_copy(grain_in, grain_ref, grain_sem),
+    ]
+    for copy in inputs:
+        copy.start()
     rows, cols = 8, 32
     row_at, col_at = lax.axis_index("row"), lax.axis_index("col")
     barrier = pltpu.get_barrier_semaphore()
@@ -102,6 +122,8 @@
         return x * PLANE + y * 3 + z
 
     perm[...] = permutation()
+    for copy in inputs:
+        copy.wait()
     phases = phases_ref[...].reshape(ROWS, YZ)
     conduct = jnp.zeros((ROWS, YZ), F32)
     for phase_id in range(PHASES):
@@ -317,7 +339,7 @@
     def along_col(s, dx, dz):
         return pltpu.make_async_remote_copy(
             src_ref=packed,
-            dst_ref=grid_ref.at[row_at, pl.ds(col_at, 1)],
+            dst_ref=inbox.at[pl.ds(col_at, 1)],
             send_sem=send_a.at[s],
             recv_sem=recv_a.at[s],
             device_id=(row_at, lax.rem(x_at + dx, 4) * 8 + lax.rem(z_at + dz, 8)),
@@ -343,7 +365,7 @@
 
     for copy in col_copies:
         copy.start()
-    grid_ref[row_at, pl.ds(col_at, 1), :] = message
+    inbox[pl.ds(col_at, 1), :] = message
 
     for c in range(3):
         for x in range(NX):
@@ -362,6 +384,7 @@
     out.start()
     for copy in col_copies:
         copy.wait_recv()
+    grid_ref[row_at] = gathered_rows(inbox, slot, sub)
     for copy in row_copies:
         copy.start()
     for copy in col_copies:
@@ -374,16 +397,17 @@
 def heavy(phases, grain, phase_cond, counts, current, load):
     smem = pl.BlockSpec(memory_space=pltpu.SMEM)
     vmem = pl.BlockSpec(memory_space=pltpu.VMEM)
+    hbm = pl.BlockSpec(memory_space=pl.ANY)
     field = pltpu.VMEM((3 * CELLS, 8, 128), F32)
     return pl.pallas_call(
         heavy_kernel,
         out_shape=(
             jax.ShapeDtypeStruct((EZ, 3, VOX, YZ), F32),
             jax.ShapeDtypeStruct((3, 3, 1, EZ), F32),
-            jax.ShapeDtypeStruct((8, 32, 128), F32),
+            jax.ShapeDtypeStruct((8, 16, 128), F32),
         ),
-        in_specs=[smem, smem, smem, smem, vmem, vmem],
-        out_specs=(pl.BlockSpec(memory_space=pl.ANY), vmem, vmem),
+        in_specs=[smem, smem, smem, smem, hbm, hbm],
+        out_specs=(hbm, vmem, vmem),
         scratch_shapes=[
             pltpu.VMEM((YZ, YZ), BF16),
             pltpu.VMEM((5, 3 * ROWS, 128), F32),
@@ -392,11 +416,16 @@
             field, field, field, field, field,
             pltpu.VMEM((3 * HALO, 8, 128), F32),
             pltpu.VMEM((1, 128), F32),
+            pltpu.VMEM((32, 128), F32),
             pltpu.VMEM((EZ, 3, VOX, YZ), F32),
+            pltpu.VMEM((EZ, VOX, YZ), jnp.int32),
+            pltpu.VMEM((EZ, VOX, YZ), F32),
             pltpu.SemaphoreType.DMA((32,)),
             pltpu.SemaphoreType.DMA((32,)),
             pltpu.SemaphoreType.DMA((8,)),
             pltpu.SemaphoreType.DMA((8,)),
+            pltpu.SemaphoreType.DMA,
+            pltpu.SemaphoreType.DMA,
             pltpu.SemaphoreType.DMA,
         ],
         compiler_params=pltpu.CompilerParams(
@@ -409,7 +438,6 @@
 def coarse_kernel(
     grid, states_in, tangent_in, states_ref, tangent_ref, increment_ref, residual_ref, states, in_sem, out_sem
 ):
-    cols = 32
     i, j = lax.axis_index("row"), lax.axis_index("col")
     inward = [pltpu.make_async_copy(states_in.at[e], states.at[e], in_sem.at[e]) for e in range(EZ)]
     outward = [pltpu.make_async_copy(states.at[e], states_ref.at[e], out_sem.at[e]) for e in range(EZ)]
@@ -420,17 +448,8 @@
     lane = lane_iota()
     slot = lane >> 3
     sub = lax.broadcasted_iota(jnp.int32, (8, 128), 0)
-    fields = [[jnp.zeros((8, 128), F32)] * 2 for _ in range(5)]
-    for col in range(cols):
-        at_col = grid[:, col, :]
-        half, place = divmod(col, 16)
-        for f in range(5):
-            spun = roll(at_col, (place - f) * 8)
-            fields[f][half] = jnp.where(slot == place, spun, fields[f][half])
+    fields = [[roll(grid[:, 2 * f + h, :], -8 * f) for h in range(2)] for f in range(5)]
     kx, ky, kz, current, load = fields
-    for before, after in zip(inward, outward):
-        before.wait()
-        after.start()
 
     def ahead_y(v):
         spun = [roll(part, -8) for part in v]
@@ -491,6 +510,10 @@
     for iteration in range(MACRO_ITERS):
         increment = [increment[h] + step * direction[h] for h in range(2)]
         residual = [residual[h] - step * image[h] for h in range(2)]
+        if iteration == 0:
+            for before, after in zip(inward, outward):
+                before.wait()
+                after.start()
         if iteration == MACRO_ITERS - 1:
             break
         applied = apply(residual)

time: 45.8 us -> 45.3 us (0.989)
  Pallas kernels: 45 us -> 44.5 us
where the time goes in v5:
time: 45.3 us; the launch traced here: 45.1 us
  Pallas kernels  44.5 us (98%)
  between operations  0.64 us (1%)
    pallas_call x1, Pallas kernels, heavy(): pl.pallas_call(heavy_kernel, out_shape=(jax.ShapeDtypeStruct((EZ, 3, VOX,...  40.2 us
    pallas_call x1, Pallas kernels, coarse(): pl.pallas_call(coarse_kernel, out_shape=(jax.ShapeDtypeStruct((EZ, 3, VOX...  4.31 us

profile of v5, /device:TPU:1, one launch (start us, length us, event | category | flops | bytes accessed | tf_op | source)
XLA Modules:
  0.0 45.1 jit_solution(2811990610422156672)
XLA Ops:
  0.6 40.2 %micro.1 = (f32[8,3,24,576]{3,2,1,0:T(8,128)}, f32[3,3,1,8]{3,2,1,0:T(1,128)}, f32[8,16,128]{2,1,0:T(8,128)}) custom-call(f32[3]{0:T(128)} %cond_ref.1, s32[8]{0:T(128)} %bitcast.15, f32[8]{0:T(128)} %bitcast.16, f32[8]{0:T(128)} %bitcast.17, s32[8,24,576]{2,1,0:T(8,128)} %bitcast.13, f32[8,24,576]{2,1,0:T(8,128)} %bitcast.14), custom_call_target="tpu_custom_call" | custom-call | tf_op jit(solution)/shard_map/micro/pallas_call | solution.py:402
  40.8 4.3 %coarse.1 = (f32[8,3,24,576]{3,2,1,0:T(8,128)}, f32[3,3,1,8]{3,2,1,0:T(1,128)}, f32[1,8]{1,0:T(1,128)}, f32[1,8]{1,0:T(1,128)}) custom-call(f32[8,16,128]{2,1,0:T(8,128)} %get-tuple-element.11.grid, f32[8,3,24,576]{3,2,1,0:T(8,128)} %get-tuple-element.12.states_in, f32[3,3,1,8]{3,2,1,0:T(1,128)} %get-tuple-element.13.tangent_in), custom_call_target="tpu_custom_call" | custom-call | tf_op jit(solution)/shard_map/coarse/pallas_call | solution.py:546

commit v6 on v5

--- a/solution.py
+++ b/solution.py
@@ -297,15 +297,22 @@
     norm = tuple(total(v) for v in norms)
     together(update(0, zero, zero))
     first = (norm, (zero,) * 3, (zero, zero), jnp.where(lane_iota() == 0, norm[2], 0.0))
-    norm, alpha, _, _ = lax.fori_loop(0, MICRO_MAX, sweep, first)
+    norm, alpha, beta, last = lax.fori_loop(0, MICRO_MAX - 1, sweep, first)
+
+    box = []
+    together(update(1, alpha[1], beta[1]), stencil(0, box))
+    norm_2 = total(last)
+    together(update(2, alpha[2], norm_2 / norm[2]), stencil(1, box))
+    together(stencil(2, box))
+    alpha = [
+        jnp.where(counts == MICRO_MAX, top / total(low), 0.0) for top, low in zip((norm[0], norm[1], norm_2), box)
+    ]
 
     inner = [[zero] * 3 for _ in range(3)]
     for t in range(CELLS):
         for c in range(3):
-            value = fluct[c * CELLS + t]
-            if c > 0:
-                value = value + alpha[c] * direct[c * CELLS + t]
-                fluct[c * CELLS + t] = value
+            value = fluct[c * CELLS + t] + alpha[c] * direct[c * CELLS + t]
+            fluct[c * CELLS + t] = value
             for d in range(3):
                 inner[d][c] = inner[d][c] + value * rhs[d * CELLS + t]
     scale = 1.0 / (VOX * YZ)
@@ -505,6 +512,7 @@
     increment = [jnp.zeros((8, 128), F32)] * 2
     applied = apply(residual)
     norm, curve = dot(residual, residual), dot(residual, applied)
+    twice = apply(applied)
     step = norm / curve
     direction, image = residual, applied
     for iteration in range(MACRO_ITERS):
@@ -516,13 +524,15 @@
                 after.start()
         if iteration == MACRO_ITERS - 1:
             break
-        applied = apply(residual)
+        applied = [applied[h] - step * twice[h] for h in range(2)]
         fresh, curve = dot(residual, residual), dot(residual, applied)
+        ahead = apply(applied)
         ratio = fresh / norm
         step = fresh / (curve - ratio * (fresh / step))
         norm = fresh
         direction = [residual[h] + ratio * direction[h] for h in range(2)]
         image = [applied[h] + ratio * image[h] for h in range(2)]
+        twice = [ahead[h] + ratio * twice[h] for h in range(2)]
 
     place = lax.rem(j, 16)
 

time: 45.3 us -> 44.7 us (0.987)
  Pallas kernels: 44.5 us -> 43.8 us
where the time goes in v6:
time: 44.7 us; the launch traced here: 44.5 us
  Pallas kernels  43.8 us (98%)
  between operations  0.64 us (1%)
    pallas_call x1, Pallas kernels, heavy(): pl.pallas_call(heavy_kernel, out_shape=(jax.ShapeDtypeStruct((EZ, 3, VOX,...  40 us
    pallas_call x1, Pallas kernels, coarse(): pl.pallas_call(coarse_kernel, out_shape=(jax.ShapeDtypeStruct((EZ, 3, VOX...  3.87 us

profile of v6, /device:TPU:1, one launch (start us, length us, event | category | flops | bytes accessed | tf_op | source)
XLA Modules:
  0.0 44.5 jit_solution(12184928525686089318)
XLA Ops:
  0.6 40.0 %micro.1 = (f32[8,3,24,576]{3,2,1,0:T(8,128)}, f32[3,3,1,8]{3,2,1,0:T(1,128)}, f32[8,16,128]{2,1,0:T(8,128)}) custom-call(f32[3]{0:T(128)} %cond_ref.1, s32[8]{0:T(128)} %bitcast.15, f32[8]{0:T(128)} %bitcast.16, f32[8]{0:T(128)} %bitcast.17, s32[8,24,576]{2,1,0:T(8,128)} %bitcast.13, f32[8,24,576]{2,1,0:T(8,128)} %bitcast.14), custom_call_target="tpu_custom_call" | custom-call | tf_op jit(solution)/shard_map/micro/pallas_call | solution.py:409
  40.6 3.9 %coarse.1 = (f32[8,3,24,576]{3,2,1,0:T(8,128)}, f32[3,3,1,8]{3,2,1,0:T(1,128)}, f32[1,8]{1,0:T(1,128)}, f32[1,8]{1,0:T(1,128)}) custom-call(f32[8,16,128]{2,1,0:T(8,128)} %get-tuple-element.11.grid, f32[8,3,24,576]{3,2,1,0:T(8,128)} %get-tuple-element.12.states_in, f32[3,3,1,8]{3,2,1,0:T(1,128)} %get-tuple-element.13.tangent_in), custom_call_target="tpu_custom_call" | custom-call | tf_op jit(solution)/shard_map/coarse/pallas_call | solution.py:556

commit v7 on v6

--- a/solution.py
+++ b/solution.py
@@ -313,18 +313,10 @@
         for c in range(3):
             value = fluct[c * CELLS + t] + alpha[c] * direct[c * CELLS + t]
             fluct[c * CELLS + t] = value
-            for d in range(3):
-                inner[d][c] = inner[d][c] + value * rhs[d * CELLS + t]
+            inner[c][c] = inner[c][c] + value * rhs[c * CELLS + t]
     scale = 1.0 / (VOX * YZ)
-    tangent = [
-        [(total(means[d] - inner[d][c]) if d == c else -total(inner[d][c])) * scale for c in range(3)]
-        for d in range(3)
-    ]
+    tangent = [[total(means[d] - inner[d][d]) * scale if d == c else None for c in range(3)] for d in range(3)]
     lane = lane_iota()
-    for d in range(3):
-        for c in range(3):
-            spread = jnp.sum(jnp.where(sub == (lane & 7), tangent[d][c], 0.0), axis=0, keepdims=True)
-            tangent_ref[d, c] = spread[:, 0:EZ]
 
     slot = lane >> 3
     message = jnp.where(slot == 0, tangent[0][0], jnp.where(slot == 1, tangent[1][1], tangent[2][2]))
@@ -373,6 +365,18 @@
     for copy in col_copies:
         copy.start()
     inbox[pl.ds(col_at, 1), :] = message
+
+    for t in range(CELLS):
+        for c in range(3):
+            value = fluct[c * CELLS + t]
+            for d in range(3):
+                if d != c:
+                    inner[d][c] = inner[d][c] + value * rhs[d * CELLS + t]
+    for d in range(3):
+        for c in range(3):
+            entry = tangent[d][c] if d == c else -total(inner[d][c]) * scale
+            spread = jnp.sum(jnp.where(sub == (lane & 7), entry, 0.0), axis=0, keepdims=True)
+            tangent_ref[d, c] = spread[:, 0:EZ]
 
     for c in range(3):
         for x in range(NX):

time: 44.7 us -> 44.5 us (level)
  no operation moved by 1% of the time
where the time goes in v7:
time: 44.5 us; the launch traced here: 44.4 us
  Pallas kernels  43.7 us (98%)
  between operations  0.64 us (1%)
    pallas_call x1, Pallas kernels, heavy(): pl.pallas_call(heavy_kernel, out_shape=(jax.ShapeDtypeStruct((EZ, 3, VOX,...  39.8 us
    pallas_call x1, Pallas kernels, coarse(): pl.pallas_call(coarse_kernel, out_shape=(jax.ShapeDtypeStruct((EZ, 3, VOX...  3.87 us

profile of v7, /device:TPU:1, one launch (start us, length us, event | category | flops | bytes accessed | tf_op | source)
XLA Modules:
  0.0 44.4 jit_solution(9109510313033876758)
XLA Ops:
  0.6 39.8 %micro.1 = (f32[8,3,24,576]{3,2,1,0:T(8,128)}, f32[3,3,1,8]{3,2,1,0:T(1,128)}, f32[8,16,128]{2,1,0:T(8,128)}) custom-call(f32[3]{0:T(128)} %cond_ref.1, s32[8]{0:T(128)} %bitcast.15, f32[8]{0:T(128)} %bitcast.16, f32[8]{0:T(128)} %bitcast.17, s32[8,24,576]{2,1,0:T(8,128)} %bitcast.13, f32[8,24,576]{2,1,0:T(8,128)} %bitcast.14), custom_call_target="tpu_custom_call" | custom-call | tf_op jit(solution)/shard_map/micro/pallas_call | solution.py:413
  40.5 3.9 %coarse.1 = (f32[8,3,24,576]{3,2,1,0:T(8,128)}, f32[3,3,1,8]{3,2,1,0:T(1,128)}, f32[1,8]{1,0:T(1,128)}, f32[1,8]{1,0:T(1,128)}) custom-call(f32[8,16,128]{2,1,0:T(8,128)} %get-tuple-element.11.grid, f32[8,3,24,576]{3,2,1,0:T(8,128)} %get-tuple-element.12.states_in, f32[3,3,1,8]{3,2,1,0:T(1,128)} %get-tuple-element.13.tangent_in), custom_call_target="tpu_custom_call" | custom-call | tf_op jit(solution)/shard_map/coarse/pallas_call | solution.py:560
